TPU v7x, 32 devices: a whole 2x2x4 slice. The times are simulated.
32 devices in a mesh: stage: 4 (over z), expert: 8 (over y, x, core).
Axes of the slice: x: 2, y: 2, z: 4, core: 2. Of those that a mesh axis runs over, the one named last changes fastest.
Arguments:
- w_gate: bfloat16 [12, 8, 1024, 512], P('stage', 'expert')
- w_up: bfloat16 [12, 8, 1024, 512], P('stage', 'expert')
- w_down: bfloat16 [12, 8, 512, 1024], P('stage', 'expert')
- hot_units: int32 [1], replicated
- slot_map: int32 [32, 2], replicated
Outputs:
- output 1: bfloat16 [12, 96, 1024, 256], P(None, ('stage', 'expert'))
- output 2: bfloat16 [12, 96, 128, 1024], P(None, ('stage', 'expert'))
All inputs are finite; a program needn't handle non-finite values.
Results may differ from a plain program's by a relative error of at most 0.001.
Values are sent between devices in bfloat16 or wider.
A program may use at most 1 GiB of HBM per device.

v0:
```python
import jax
import jax.numpy as jnp
from jax import lax
from jax.sharding import PartitionSpec as P


def solution(mesh):
    stage_count = mesh.shape['stage']
    group_count = mesh.shape['expert']
    devices_flat = stage_count * group_count
    flat_axes = ('stage', 'expert')
    perm_pairs = [(stage_idx * group_count + rank_idx, rank_idx * stage_count + stage_idx) for stage_idx in range(stage_count) for rank_idx in range(group_count)]

    def local_handover(gate_blk, up_blk, down_blk, hot_units, slot_map):
        layers_stage, experts_rank, d_model, ff_expert = gate_blk.shape
        layers = layers_stage * stage_count
        experts = experts_rank * group_count
        split_count = max(devices_flat // experts, 1)
        units_dev = max(experts // devices_flat, 1)
        ff_dev = ff_expert // split_count
        gate_parts = gate_blk.reshape(layers_stage, experts_rank, d_model, split_count, ff_dev)
        up_parts = up_blk.reshape(layers_stage, experts_rank, d_model, split_count, ff_dev)
        fused_send = jnp.concatenate([gate_parts, up_parts], axis=-1).transpose(0, 1, 3, 2, 4).reshape(layers_stage, stage_count, units_dev, d_model, 2 * ff_dev)
        down_send = down_blk.reshape(layers_stage, stage_count, units_dev, ff_dev, d_model)
        fused_recv = lax.all_to_all(fused_send, 'stage', 1, 0, tiled=True).reshape(layers, units_dev, d_model, 2 * ff_dev)
        down_recv = lax.all_to_all(down_send, 'stage', 1, 0, tiled=True).reshape(layers, units_dev, ff_dev, d_model)
        fused_home = lax.ppermute(fused_recv, flat_axes, perm_pairs)
        down_home = lax.ppermute(down_recv, flat_axes, perm_pairs)
        my_flat = lax.axis_index('stage') * group_count + lax.axis_index('expert')
        owned_mask = (hot_units // units_dev == my_flat)[None, :, None, None]
        local_pick = hot_units % units_dev
        fused_hot = lax.psum(jnp.where(owned_mask, jnp.take(fused_home, local_pick, axis=1), 0), flat_axes)
        down_hot = lax.psum(jnp.where(owned_mask, jnp.take(down_home, local_pick, axis=1), 0), flat_axes)
        my_slots = lax.dynamic_index_in_dim(slot_map, my_flat, axis=0, keepdims=False)
        slot_used = (my_slots >= 0)[None, :, None, None]
        hot_pick = jnp.maximum(my_slots, 0)
        fused_extra = jnp.where(slot_used, jnp.take(fused_hot, hot_pick, axis=1), 0)
        down_extra = jnp.where(slot_used, jnp.take(down_hot, hot_pick, axis=1), 0)
        return jnp.concatenate([fused_home, fused_extra], axis=1), jnp.concatenate([down_home, down_extra], axis=1)

    return jax.shard_map(local_handover, mesh=mesh, in_specs=(P('stage', 'expert'), P('stage', 'expert'), P('stage', 'expert'), P(), P()), out_specs=(P(None, flat_axes), P(None, flat_axes)), check_vma=False)
```

profile of v0, /device:TPU:2, one launch (start us, length us, event | category | flops | bytes accessed | tf_op | source)
XLA Modules:
  0.0 1064.4 jit_solution(3286388267465281295)
XLA Ops:
  7.2 3.2 copy.12
  10.4 4.6 copy.13
  15.0 5.3 maximum_bitcast_fusion
  20.3 8.7 copy.14
  29.0 0.0 copy-start.1
  29.0 5.5 all-to-all-start
  34.5 0.0 copy-done.1
  34.5 2.0 copy.16
  36.4 136.0 %all-to-all-done = bf16[3,4,1,1024,256]{4,3,0,2,1:T(8,128)(2,1)} async-done(((bf16[3,4,1,1024,256]{4,3,0,2,1:T(8,128)(2,1)}), bf16[3,4,1,1024,256]{4,3,0,2,1:T(8,128)(2,1)}, u32[]{:S(2)}, u32[]{:S(2)}) %all-to-all-start) | async-done | bytes 6291488 | tf_op jit(solution)/shard_map/all_to_all | solution.py:25
  172.5 3.7 all-to-all-start.1
  176.2 0.0 all-reduce.3.cloned.1.call-start
  176.2 3.8 collective-permute-start
  180.0 235.6 %all-to-all-done.1 = bf16[3,4,1,128,1024]{4,3,0,2,1:T(8,128)(2,1)S(1)} async-done(((bf16[3,4,1,128,1024]{4,3,0,2,1:T(8,128)(2,1)}), bf16[3,4,1,128,1024]{4,3,0,2,1:T(8,128)(2,1)S(1)}, u32[]{:S(2)}, u32[]{:S(2)}) %all-to-all-start.1) | async-done | bytes 3145760 | tf_op jit(solution)/shard_map/all_to_all | solution.py:26
  415.6 0.0 copy-start.2
  415.6 1.7 copy-done.2
  417.3 1.9 collective-permute-start.1
  419.8 234.0 %collective-permute-done.1 = bf16[12,1,128,1024]{3,2,1,0:T(8,128)(2,1)S(1)} collective-permute-done((bf16[12,1,128,1024]{3,2,1,0:T(8,128)(2,1)}, bf16[12,1,128,1024]{3,2,1,0:T(8,128)(2,1)S(1)}, u32[]{:S(2)}, u32[]{:S(2)}) %collective-permute-start.1) | collective-permute-done | bytes 3145760 | tf_op jit(solution)/shard_map/ppermute | solution.py:28
  653.9 1.9 broadcast_select_fusion.1
  655.8 0.0 collective-permute-done
  655.8 3.1 broadcast_select_fusion
  658.9 0.0 copy-start.3
  658.9 0.0 all-reduce.3.cloned.1.call-update
  658.9 0.7 copy-done.3
  659.6 0.2 compare_reduce_fusion.1
  659.7 371.1 %all-reduce.3.cloned.1.call-done = (bf16[12,1,1024,256]{3,2,1,0:T(8,128)(2,1)}, bf16[12,1,128,1024]{3,2,1,0:T(8,128)(2,1)}) async-done(((bf16[12,1,1024,256]{3,2,1,0:T(8,128)(2,1)}, bf16[12,1,128,1024]{3,2,1,0:T(8,128)(2,1)}), (bf16[12,1,1024,256]{3,2,1,0:T(8,128)(2,1)}, bf16[12,1,128,1024]{3,2,1,0:T(8,128)(2,1)})) %all-reduce.3.cloned.1.call-update) | async-done | bytes 9437200 | tf_op jit(solution)/shard_map/psum | solution.py:32
  1030.9 0.0 copy-start
  1030.9 5.2 select_select_fusion
  1036.1 0.0 copy-done
  1036.1 3.3 select_select_fusion.1
  1039.5 10.8 %pad_maximum_fusion = bf16[12,3,1024,256]{3,2,1,0:T(8,128)(2,1)} fusion(bf16[12,2,1024,256]{3,2,1,0:T(8,128)(2,1)S(1)} %select_select_fusion, bf16[12,1,1024,256]{3,2,1,0:T(8,128)(2,1)} %collective-permute-done), kind=kLoop, calls=%fused_computation | loop fusion | flops 9437184 | bytes 37748736 | tf_op jit(solution)/shard_map/concatenate | solution.py:39
  1050.2 7.3 pad_maximum_fusion.1
Async XLA Ops:
  29.0 5.5 copy-start.1
  29.0 143.5 %all-to-all-start = ((bf16[3,4,1,1024,256]{4,3,0,2,1:T(8,128)(2,1)}), bf16[3,4,1,1024,256]{4,3,0,2,1:T(8,128)(2,1)}, u32[]{:S(2)}, u32[]{:S(2)}) async-start(bf16[3,4,1,1024,256]{4,3,0,2,1:T(8,128)(2,1)} %copy.14), calls=%async_computation | async-start | bytes 12582912 | tf_op jit(solution)/shard_map/all_to_all | solution.py:25
  172.5 243.2 %all-to-all-start.1 = ((bf16[3,4,1,128,1024]{4,3,0,2,1:T(8,128)(2,1)}), bf16[3,4,1,128,1024]{4,3,0,2,1:T(8,128)(2,1)S(1)}, u32[]{:S(2)}, u32[]{:S(2)}) async-start(bf16[3,4,1,128,1024]{4,3,0,2,1:T(8,128)(2,1)} %copy.16), calls=%async_computation.1 | async-start | bytes 6291456 | tf_op jit(solution)/shard_map/all_to_all | solution.py:26
  176.2 854.7 %all-reduce.3.cloned.1.call-start = ((), (), s32[]{:S(2)}) async-start(), calls=%async_computation.2 | async-start | bytes 18874368 | tf_op jit(solution)/shard_map/psum | solution.py:32
  176.2 479.5 %collective-permute-start = (bf16[12,1,1024,256]{3,2,1,0:T(8,128)(2,1)}, bf16[12,1,1024,256]{3,2,1,0:T(8,128)(2,1)}, u32[]{:S(2)}, u32[]{:S(2)}) collective-permute-start(bf16[12,1,1024,256]{3,2,1,0:T(8,128)(2,1)} %bitcast.7), channel_id=1, source_target_pairs={{0,0},{1,4},{2,8},{3,12},{4,16},{5,20},{6,24},{7,28},{8,1},{9,5},{... | collective-permute-start | bytes 18874376 | tf_op jit(solution)/shard_map/ppermute | solution.py:27
  415.6 1.7 copy-start.2
  417.3 236.6 %collective-permute-start.1 = (bf16[12,1,128,1024]{3,2,1,0:T(8,128)(2,1)}, bf16[12,1,128,1024]{3,2,1,0:T(8,128)(2,1)S(1)}, u32[]{:S(2)}, u32[]{:S(2)}) collective-permute-start(bf16[12,1,128,1024]{3,2,1,0:T(8,128)(2,1)} %bitcast.30), channel_id=1, source_target_pairs={{0,0},{1,4},{2,8},{3,12},{4,16},{5,20},{6,24},{7,28},{8,1},{9,5},{... | collective-permute-start | bytes 9437192 | tf_op jit(solution)/shard_map/ppermute | solution.py:28
  658.9 0.7 copy-start.3
  1030.9 5.2 copy-start
Sparse Core Ops, SparseCore 0:
  659.0 371.8 all-reduce.2
where the time goes:
time: 1070 us; the launch traced here: 1060 us
  waiting for transfers between devices  977 us (91%)
  other arithmetic  37.1 us (3%)
  local copies, waits for them, and re-layouts  20.8 us (2%)
  starting transfers between devices  14.9 us (1%)
  between operations  14.8 us (1%)
    psum x1, waiting for transfers between devices, local_handover(): lax.psum(jnp.where(owned_mask, jnp.take(fused_home, local_pick, axis=1),...  371 us
    all_to_all x1, waiting for transfers between devices, local_handover(): lax.all_to_all(down_send, 'stage', 1, 0, tiled=True)  236 us
    ppermute x1, waiting for transfers between devices, local_handover(): down_home = lax.ppermute(down_recv, flat_axes, perm_pairs)  234 us
    all_to_all x1, waiting for transfers between devices, local_handover(): lax.all_to_all(fused_send, 'stage', 1, 0, tiled=True)  136 us
  transfers between devices with their start and end apart: 5, of which 4 were waited for; matrix products, arithmetic and copies ran while one was open for 0% of the time, Pallas kernels for 0%

commit v1 on v0

v1 whole, which is shorter than its diff:
```python
import functools

import jax
import jax.numpy as jnp
from jax import lax
from jax.experimental import pallas as pl
from jax.experimental.pallas import tpu as pltpu
from jax.sharding import PartitionSpec as P

MESH = pl.DeviceIdType.MESH
BF16 = jnp.bfloat16


def exchange_kernel(dims, hot_ref, gate, up, down, home13, homed, hot13, hotd,
                    part_g, part_u, part_d, cand13, candd, rel13, reld, got13, gotd, sel13, seld,
                    s_own, s_p1, s_z, s_hs, s_hz, s_hp,
                    r_rel, r_home, r_hs, r_hz, r_hp, l_own, l_rel, l_part, l_hot):
    nl, dm, ff = dims
    z = lax.axis_index('stage')
    j = lax.axis_index('expert')
    y, x, c = j // 4, (j // 2) % 2, j % 2
    zt = j // 2
    r8 = dm // 8
    d8 = ff // 8

    def dev(zz, yy, xx, cc):
        return (zz, 4 * yy + 2 * xx + cc)

    def rdma(src, dst, ss, rs, to):
        return pltpu.make_async_remote_copy(src_ref=src, dst_ref=dst, send_sem=ss, recv_sem=rs,
                                            device_id=to, device_id_type=MESH)

    def landed(ref, sem):
        rdma(ref, ref, sem, sem, (z, j)).wait_recv()

    def cols(k):
        return pl.ds(pl.multiple_of(k * ff, ff), ff)

    def pieces(t, k, dst13, dstd):
        return ((gate.at[t, 0, :, cols(k)], dst13.at[:, pl.ds(0, ff)]),
                (up.at[t, 0, :, cols(k)], dst13.at[:, pl.ds(ff, ff)]),
                (down.at[t, 0, cols(k), :], dstd))

    def own(t, do_local, do_remote):
        lay = nl * z + t
        for kc in range(2):
            k = 2 * x + kc
            todo = pieces(t, k, home13.at[lay], homed.at[lay])
            stays = jnp.logical_and(z == zt, c == kc)

            @pl.when(jnp.logical_and(c == y, stays))
            def _():
                for a, (src, dst) in enumerate(todo):
                    do_local(pltpu.make_async_copy(src, dst, l_own.at[t, a]))

            @pl.when(jnp.logical_and(c == y, jnp.logical_not(stays)))
            def _():
                for a, (src, dst) in enumerate(todo):
                    do_remote(rdma(src, dst, s_own.at[kc, t, a], r_home.at[lay, a // 2], dev(zt, y, x, kc)))

    def p1(t, do):
        def to(dx, m, slot):
            xx = (x + dx) % 2
            for kc in range(2):
                for a, (src, dst) in enumerate(pieces(t, 2 * xx + kc, rel13.at[m, t], reld.at[m, t])):
                    do(rdma(src, dst, s_p1.at[slot, kc, t, a], r_rel.at[m, t, a // 2], dev(z, c, xx, kc)))

        @pl.when(c == y)
        def _():
            to(1, 0, 0)

        @pl.when(c != y)
        def _():
            to(0, 1, 0)
            to(1, 2, 1)

    relays = ((2 * y + 1 - x), (2 * (1 - y) + x), (2 * (1 - y) + 1 - x))

    def zsend(t, wait, do_local, do_remote):
        lay = nl * z + t
        for m in range(3):
            zm = relays[m]
            src = (rel13.at[m, t], reld.at[m, t])
            dst = (home13.at[lay], homed.at[lay])
            if wait:
                for a in range(2):
                    landed(src[a], r_rel.at[m, t, a])

            @pl.when(zm == z)
            def _():
                for a in range(2):
                    do_local(pltpu.make_async_copy(src[a], dst[a], l_rel.at[t, a]))

            @pl.when(zm != z)
            def _():
                for a in range(2):
                    do_remote(rdma(src[a], dst[a], s_z.at[m, t, a], r_home.at[lay, a], (zm, j)))

    start = lambda cp: cp.start()
    wait_send = lambda cp: cp.wait_send()
    wait = lambda cp: cp.wait()
    skip = lambda cp: None

    def part_loads():
        for k in range(4):
            yield pltpu.make_async_copy(gate.at[:, 0, :, pl.ds(k * ff, ff)], part_g.at[k], l_part.at[k, 0])
            yield pltpu.make_async_copy(up.at[:, 0, :, pl.ds(k * ff, ff)], part_u.at[k], l_part.at[k, 1])
            yield pltpu.make_async_copy(down.at[:, 0, pl.ds(k * ff, ff), :], part_d.at[k], l_part.at[k, 2])

    def rows13(q):
        return pl.ds(pl.multiple_of(q * r8, r8), r8)

    def rowsd(q):
        return pl.ds(pl.multiple_of(q * d8, d8), d8)

    def scatter_local():
        yield pltpu.make_async_copy(cand13.at[:, rows13(j), :], got13.at[j], l_hot.at[0])
        yield pltpu.make_async_copy(candd.at[:, rowsd(j), :], gotd.at[j], l_hot.at[1])

    def scatter():
        for d in range(1, 8):
            q = (j + d) % 8
            yield rdma(cand13.at[:, rows13(q), :], got13.at[j], s_hs.at[d, 0], r_hs.at[j, 0], (z, q))
            yield rdma(candd.at[:, rowsd(q), :], gotd.at[j], s_hs.at[d, 1], r_hs.at[j, 1], (z, q))

    def hot_piece(zz, q):
        ls = pl.ds(nl * zz, nl)
        return hot13.at[ls, rows13(q), :], hotd.at[ls, rowsd(q), :]

    def hot_rows(q):
        return hot13.at[:, rows13(q), :], hotd.at[:, rowsd(q), :]

    z1 = z + 1 - 2 * (z % 2)
    zc = 3 - z
    zf = 3 - z1

    def sel_local():
        p13, pd = hot_piece(z, j)
        yield pltpu.make_async_copy(sel13, p13, l_hot.at[2])
        yield pltpu.make_async_copy(seld, pd, l_hot.at[3])

    def along_z():
        p13, pd = hot_piece(z, j)
        for i, to in enumerate((zc, z1)):
            yield rdma(sel13, p13, s_hz.at[i, 0], r_hz.at[z, 0], (to, j))
            yield rdma(seld, pd, s_hz.at[i, 1], r_hz.at[z, 1], (to, j))

    def forward_z():
        p13, pd = hot_piece(zc, j)
        yield rdma(p13, p13, s_hz.at[2, 0], r_hz.at[zc, 0], (z1, j))
        yield rdma(pd, pd, s_hz.at[2, 1], r_hz.at[zc, 1], (z1, j))

    def hot_z_landed(zz):
        for a, ref in enumerate(hot_piece(zz, j)):
            landed(ref, r_hz.at[zz, a])

    same_core = ((y, 1 - x), (1 - y, x), (1 - y, 1 - x))

    def gather():
        p13, pd = hot_rows(j)
        for i, (yy, xx) in enumerate(same_core):
            yield rdma(p13, p13, s_hp.at[i, 0], r_hp.at[j, 0], dev(z, yy, xx, c))
            yield rdma(pd, pd, s_hp.at[i, 1], r_hp.at[j, 1], dev(z, yy, xx, c))
        yield rdma(p13, p13, s_hp.at[3, 0], r_hp.at[j, 0], dev(z, y, x, 1 - c))
        yield rdma(pd, pd, s_hp.at[3, 1], r_hp.at[j, 1], dev(z, y, x, 1 - c))

    def hot_rows_landed(q):
        for a, ref in enumerate(hot_rows(q)):
            landed(ref, r_hp.at[q, a])

    def to_sibling(i):
        yy, xx = same_core[i]
        q = 4 * yy + 2 * xx + c
        p13, pd = hot_rows(q)
        yield rdma(p13, p13, s_hp.at[4 + i, 0], r_hp.at[q, 0], dev(z, y, x, 1 - c))
        yield rdma(pd, pd, s_hp.at[4 + i, 1], r_hp.at[q, 1], dev(z, y, x, 1 - c))

    own(0, start, start)
    p1(0, start)
    for cp in part_loads():
        cp.start()
    for cp in part_loads():
        cp.wait()
    kh = lax.rem(hot_ref[0], 4)
    eh = lax.div(hot_ref[0], 4)

    def build(i, carry):
        t, b = i // 8, i % 8
        rr = pl.ds(pl.multiple_of(b * r8, r8), r8)
        rd = pl.ds(pl.multiple_of(b * d8, d8), d8)
        cand13[t, rr, 0:ff] = part_g[kh, t, rr, :]
        cand13[t, rr, ff:2 * ff] = part_u[kh, t, rr, :]
        candd[t, rd, :] = part_d[kh, t, rd, :]
        return carry

    lax.fori_loop(0, nl * 8, build, 0)
    p1(1, start)
    for cp in scatter_local():
        cp.start()
    for cp in scatter():
        cp.start()
    p1(2, start)

    zsend(0, True, start, start)
    for cp in scatter_local():
        cp.wait()
    for d in range(1, 8):
        q = (j + d) % 8
        landed(got13.at[q], r_hs.at[q, 0])
        landed(gotd.at[q], r_hs.at[q, 1])
    sel13[...] = got13[eh]
    seld[...] = gotd[eh]
    own(1, start, start)
    for cp in sel_local():
        cp.start()
    for cp in along_z():
        cp.start()
    zsend(1, True, start, start)
    hot_z_landed(zc)
    for cp in forward_z():
        cp.start()
    own(2, start, start)
    zsend(2, True, start, start)

    for cp in sel_local():
        cp.wait()
    hot_z_landed(z1)
    hot_z_landed(zf)
    for cp in gather():
        cp.start()
    for i in range(3):
        yy, xx = same_core[i]
        hot_rows_landed(4 * yy + 2 * xx + c)
        for cp in to_sibling(i):
            cp.start()

    for yy in range(2):
        for xx in range(2):
            hot_rows_landed(4 * yy + 2 * xx + 1 - c)
    for zz in range(4):
        for t in range(nl):
            lay = nl * zz + t
            away = z != zz
            sib = jnp.logical_and(z == zt, c != y)

            @pl.when(jnp.logical_or(away, sib))
            def _():
                landed(home13.at[lay], r_home.at[lay, 0])
                landed(homed.at[lay], r_home.at[lay, 1])

    for t in range(nl):
        own(t, wait, wait_send)
        p1(t, wait_send)
        zsend(t, False, wait, wait_send)
    for group in (scatter(), along_z(), forward_z(), gather(), to_sibling(0), to_sibling(1), to_sibling(2)):
        for cp in group:
            cp.wait_send()


def place_kernel(slots_ref, home13, homed, hot13, hotd, w13, wd, zero13, zerod, sem):
    n = lax.axis_index('stage') * 8 + lax.axis_index('expert')
    nlay = home13.shape[0]

    def home():
        yield pltpu.make_async_copy(home13, w13.at[:, 0], sem.at[0, 0])
        yield pltpu.make_async_copy(homed, wd.at[:, 0], sem.at[0, 1])

    for cp in home():
        cp.start()
    zero13[...] = jnp.zeros_like(zero13)
    zerod[...] = jnp.zeros_like(zerod)

    def fill(act):
        for h in range(2):
            used = slots_ref[n, h] >= 0

            @pl.when(used)
            def _():
                act(pltpu.make_async_copy(hot13, w13.at[:, 1 + h], sem.at[1 + h, 0]))
                act(pltpu.make_async_copy(hotd, wd.at[:, 1 + h], sem.at[1 + h, 1]))

            @pl.when(jnp.logical_not(used))
            def _():
                for lay in range(nlay):
                    act(pltpu.make_async_copy(zero13, w13.at[lay, 1 + h], sem.at[3 + h, 2 * lay]))
                    act(pltpu.make_async_copy(zerod, wd.at[lay, 1 + h], sem.at[3 + h, 2 * lay + 1]))

    fill(lambda cp: cp.start())
    fill(lambda cp: cp.wait())
    for cp in home():
        cp.wait()


def solution(mesh):
    flat = ('stage', 'expert')
    any_spec = pl.BlockSpec(memory_space=pl.ANY)
    smem = pl.BlockSpec(memory_space=pltpu.SMEM)
    vmem = pl.BlockSpec(memory_space=pltpu.VMEM)

    def body(gate, up, down, hot_units, slot_map):
        nl, _, dm, f4 = gate.shape
        ff = f4 // 4
        lay = nl * 4
        dma = pltpu.SemaphoreType.DMA
        shapes = [(lay, dm, 2 * ff), (lay, ff, dm)] * 2
        outs = pl.pallas_call(
            functools.partial(exchange_kernel, (nl, dm, ff)),
            out_shape=[pltpu.VMEM(s, BF16) for s in shapes],
            in_specs=[smem, any_spec, any_spec, any_spec],
            out_specs=[vmem] * 4,
            scratch_shapes=[
                pltpu.VMEM((4, nl, dm, ff), BF16), pltpu.VMEM((4, nl, dm, ff), BF16), pltpu.VMEM((4, nl, ff, dm), BF16),
                pltpu.VMEM((nl, dm, 2 * ff), BF16), pltpu.VMEM((nl, ff, dm), BF16),
                pltpu.VMEM((3, nl, dm, 2 * ff), BF16), pltpu.VMEM((3, nl, ff, dm), BF16),
                pltpu.VMEM((8, nl, dm // 8, 2 * ff), BF16), pltpu.VMEM((8, nl, ff // 8, dm), BF16),
                pltpu.VMEM((nl, dm // 8, 2 * ff), BF16), pltpu.VMEM((nl, ff // 8, dm), BF16),
                dma((2, nl, 3)), dma((2, 2, nl, 3)), dma((3, nl, 2)), dma((8, 2)), dma((3, 2)), dma((7, 2)),
                dma((3, nl, 2)), dma((lay, 2)), dma((8, 2)), dma((4, 2)), dma((8, 2)),
                dma((nl, 3)), dma((nl, 2)), dma((4, 3)), dma((4,)),
            ],
            compiler_params=pltpu.CompilerParams(has_side_effects=True, vmem_limit_bytes=44 << 20),
            name='exchange',
        )(hot_units, gate, up, down)
        return pl.pallas_call(
            place_kernel,
            out_shape=[jax.ShapeDtypeStruct((lay, 3, dm, 2 * ff), BF16), jax.ShapeDtypeStruct((lay, 3, ff, dm), BF16)],
            in_specs=[smem] + [vmem] * 4,
            out_specs=[any_spec] * 2,
            scratch_shapes=[pltpu.VMEM((dm, 2 * ff), BF16), pltpu.VMEM((ff, dm), BF16), dma((5, 2 * lay))],
            compiler_params=pltpu.CompilerParams(vmem_limit_bytes=20 << 20),
            name='place',
        )(slot_map, *outs)

    specs = P('stage', 'expert')
    return jax.shard_map(body, mesh=mesh, in_specs=(specs, specs, specs, P(), P()),
                         out_specs=(P(None, flat), P(None, flat)), check_vma=False)
```

time: 1070 us -> 272 us (0.25)
  the two profiles are of different devices: /device:TPU:2 before, /device:TPU:7 now
where the time goes in v1:
time: 272 us; the launch traced here: 271 us
  Pallas kernels  269 us (99%)
    pallas_call x1, Pallas kernels, body(): pl.pallas_call(functools.partial(exchange_kernel, (nl, dm, ff)), out_shap...  258 us
    pallas_call x1, Pallas kernels, body(): pl.pallas_call(place_kernel, out_shape=[jax.ShapeDtypeStruct((lay, 3, dm,...  11.3 us

profile of v1, /device:TPU:7, one launch (start us, length us, event | category | flops | bytes accessed | tf_op | source)
XLA Modules:
  0.0 271.4 jit_solution(12884075261602072625)
XLA Ops:
  1.3 0.8 copy.7.slots_ref
  2.0 258.1 %exchange.1 = (bf16[12,1024,256]{2,1,0:T(8,128)(2,1)S(1)}, bf16[12,128,1024]{2,1,0:T(8,128)(2,1)S(1)}, bf16[12,1024,256]{2,1,0:T(8,128)(2,1)S(1)}, bf16[12,128,1024]{2,1,0:T(8,128)(2,1)S(1)}) custom-call(s32[1]{0:T(128)S(6)} %copy.8.hot_ref, bf16[3,1,1024,512]{3,2,1,0:T(8,128)(2,1)} %gate.1, bf16[3,1,1024,512]{3,2,1,0:T(8,128)(2,1)} %up.1, ...), custom_call_target="tpu_custom_call" | custom-call | tf_op jit(solution)/shard_map/exchange/pallas_call | solution.py:306
  260.1 11.3 %place.1 = (bf16[12,3,1024,256]{3,2,1,0:T(8,128)(2,1)}, bf16[12,3,128,1024]{3,2,1,0:T(8,128)(2,1)}) custom-call(s32[32,2]{1,0:T(8,128)S(1)} %copy.7.slots_ref, bf16[12,1024,256]{2,1,0:T(8,128)(2,1)S(1)} %get-tuple-element.6.home13, bf16[12,128,1024]{2,1,0:T(8,128)(2,1)S(1)} %get-tuple-element.7.homed, bf16[12,1024,256]{2,1,0:T(8,128)(2,1)S(1)} %get-tuple-element.8.hot13, ...), custom_call_target="tpu_custom_call" | custom-call | tf_op jit(solution)/shard_map/place/pallas_call | solution.py:324

commit v2 on v1

--- a/solution.py
+++ b/solution.py
@@ -8,13 +8,20 @@
 from jax.sharding import PartitionSpec as P
 
 MESH = pl.DeviceIdType.MESH
+ORDER = (
+    'load', 'own0', 'in00', 'in01', 'build', 'in02', 'in03', 'pair', 'z00', 'merge', 'scatter', 'in10', 'in11',
+    'in12', 'in13', 'in20', 'in21', 'in22', 'in23', 'z01', 'z02', 'z03', 'select', 'alongz', 'own1', 'z10', 'z11',
+    'fwd', 'z12', 'z13', 'own2', 'gather', 'z20', 'z21', 'z22', 'z23', 'sib',
+)
+CUTS = (((0, 1), (1, 1), (2, 2), (4, 4)), ((0, 2), (2, 2), (4, 2), (6, 2)), ((0, 2), (2, 2), (4, 2), (6, 2)))
 BF16 = jnp.bfloat16
 
 
 def exchange_kernel(dims, hot_ref, gate, up, down, home13, homed, hot13, hotd,
-                    part_g, part_u, part_d, cand13, candd, rel13, reld, got13, gotd, sel13, seld,
-                    s_own, s_p1, s_z, s_hs, s_hz, s_hp,
-                    r_rel, r_home, r_hs, r_hz, r_hp, l_own, l_rel, l_part, l_hot):
+                    part_g, part_u, part_d, pair13, paird, give13, gived, mine13, mined, rel13, reld,
+                    got13, gotd, sel13, seld,
+                    s_own, s_p1, s_z, s_pair, s_hs, s_hz, s_hp,
+                    r_rel, r_home, r_pair, r_hs, r_hz, r_hp, l_own, l_rel, l_part, l_hot):
     nl, dm, ff = dims
     z = lax.axis_index('stage')
     j = lax.axis_index('expert')
@@ -58,12 +65,22 @@
                 for a, (src, dst) in enumerate(todo):
                     do_remote(rdma(src, dst, s_own.at[kc, t, a], r_home.at[lay, a // 2], dev(zt, y, x, kc)))
 
-    def p1(t, do):
+    def rows(t, p):
+        e0, n = CUTS[t][p]
+        return pl.ds(e0 * r8, n * r8), pl.ds(e0 * d8, n * d8)
+
+    def p1(t, p, do):
+        r13, rd = rows(t, p)
+
         def to(dx, m, slot):
             xx = (x + dx) % 2
             for kc in range(2):
-                for a, (src, dst) in enumerate(pieces(t, 2 * xx + kc, rel13.at[m, t], reld.at[m, t])):
-                    do(rdma(src, dst, s_p1.at[slot, kc, t, a], r_rel.at[m, t, a // 2], dev(z, c, xx, kc)))
+                k = 2 * xx + kc
+                todo = ((gate.at[t, 0, r13, cols(k)], rel13.at[m, t, r13, pl.ds(0, ff)]),
+                        (up.at[t, 0, r13, cols(k)], rel13.at[m, t, r13, pl.ds(ff, ff)]),
+                        (down.at[t, 0, pl.ds(pl.multiple_of(k * ff + rd.start, d8), rd.size), :], reld.at[m, t, rd]))
+                for a, (src, dst) in enumerate(todo):
+                    do(rdma(src, dst, s_p1.at[slot, kc, t, p, a], r_rel.at[m, t, p, a // 2], dev(z, c, xx, kc)))
 
         @pl.when(c == y)
         def _():
@@ -76,30 +93,30 @@
 
     relays = ((2 * y + 1 - x), (2 * (1 - y) + x), (2 * (1 - y) + 1 - x))
 
-    def zsend(t, wait, do_local, do_remote):
+    def zsend(t, p, ms, wait, do_local, do_remote):
         lay = nl * z + t
-        for m in range(3):
+        r13, rd = rows(t, p)
+        for m in ms:
             zm = relays[m]
-            src = (rel13.at[m, t], reld.at[m, t])
-            dst = (home13.at[lay], homed.at[lay])
+            src = (rel13.at[m, t, r13], reld.at[m, t, rd])
+            dst = (home13.at[lay, r13], homed.at[lay, rd])
             if wait:
                 for a in range(2):
-                    landed(src[a], r_rel.at[m, t, a])
+                    landed(src[a], r_rel.at[m, t, p, a])
 
             @pl.when(zm == z)
             def _():
                 for a in range(2):
-                    do_local(pltpu.make_async_copy(src[a], dst[a], l_rel.at[t, a]))
+                    do_local(pltpu.make_async_copy(src[a], dst[a], l_rel.at[t, p, a]))
 
             @pl.when(zm != z)
             def _():
                 for a in range(2):
-                    do_remote(rdma(src[a], dst[a], s_z.at[m, t, a], r_home.at[lay, a], (zm, j)))
+                    do_remote(rdma(src[a], dst[a], s_z.at[m, t, p, a], r_home.at[lay, a], (zm, j)))
 
     start = lambda cp: cp.start()
     wait_send = lambda cp: cp.wait_send()
     wait = lambda cp: cp.wait()
-    skip = lambda cp: None
 
     def part_loads():
         for k in range(4):
@@ -113,15 +130,24 @@
     def rowsd(q):
         return pl.ds(pl.multiple_of(q * d8, d8), d8)
 
+    chip = j // 2
+
+    def pair():
+        to = dev(z, y, x, 1 - c)
+        yield rdma(give13, pair13.at[c], s_pair.at[0], r_pair.at[0], to)
+        yield rdma(gived, paird.at[c], s_pair.at[1], r_pair.at[1], to)
+
     def scatter_local():
-        yield pltpu.make_async_copy(cand13.at[:, rows13(j), :], got13.at[j], l_hot.at[0])
-        yield pltpu.make_async_copy(candd.at[:, rowsd(j), :], gotd.at[j], l_hot.at[1])
+        yield pltpu.make_async_copy(mine13.at[chip], got13.at[chip], l_hot.at[0])
+        yield pltpu.make_async_copy(mined.at[chip], gotd.at[chip], l_hot.at[1])
+
+    same_core = ((y, 1 - x), (1 - y, x), (1 - y, 1 - x))
 
     def scatter():
-        for d in range(1, 8):
-            q = (j + d) % 8
-            yield rdma(cand13.at[:, rows13(q), :], got13.at[j], s_hs.at[d, 0], r_hs.at[j, 0], (z, q))
-            yield rdma(candd.at[:, rowsd(q), :], gotd.at[j], s_hs.at[d, 1], r_hs.at[j, 1], (z, q))
+        for i, (yy, xx) in enumerate(same_core):
+            q = 2 * yy + xx
+            yield rdma(mine13.at[q], got13.at[chip], s_hs.at[i, 0], r_hs.at[chip, 0], dev(z, yy, xx, c))
+            yield rdma(mined.at[q], gotd.at[chip], s_hs.at[i, 1], r_hs.at[chip, 1], dev(z, yy, xx, c))
 
     def hot_piece(zz, q):
         ls = pl.ds(nl * zz, nl)
@@ -153,8 +179,6 @@
     def hot_z_landed(zz):
         for a, ref in enumerate(hot_piece(zz, j)):
             landed(ref, r_hz.at[zz, a])
-
-    same_core = ((y, 1 - x), (1 - y, x), (1 - y, 1 - x))
 
     def gather():
         p13, pd = hot_rows(j)
@@ -175,64 +199,87 @@
         yield rdma(p13, p13, s_hp.at[4 + i, 0], r_hp.at[q, 0], dev(z, y, x, 1 - c))
         yield rdma(pd, pd, s_hp.at[4 + i, 1], r_hp.at[q, 1], dev(z, y, x, 1 - c))
 
-    own(0, start, start)
-    p1(0, start)
-    for cp in part_loads():
-        cp.start()
-    for cp in part_loads():
-        cp.wait()
-    kh = lax.rem(hot_ref[0], 4)
-    eh = lax.div(hot_ref[0], 4)
-
-    def build(i, carry):
-        t, b = i // 8, i % 8
-        rr = pl.ds(pl.multiple_of(b * r8, r8), r8)
-        rd = pl.ds(pl.multiple_of(b * d8, d8), d8)
-        cand13[t, rr, 0:ff] = part_g[kh, t, rr, :]
-        cand13[t, rr, ff:2 * ff] = part_u[kh, t, rr, :]
-        candd[t, rd, :] = part_d[kh, t, rd, :]
-        return carry
-
-    lax.fori_loop(0, nl * 8, build, 0)
-    p1(1, start)
-    for cp in scatter_local():
-        cp.start()
-    for cp in scatter():
-        cp.start()
-    p1(2, start)
-
-    zsend(0, True, start, start)
-    for cp in scatter_local():
-        cp.wait()
-    for d in range(1, 8):
-        q = (j + d) % 8
-        landed(got13.at[q], r_hs.at[q, 0])
-        landed(gotd.at[q], r_hs.at[q, 1])
-    sel13[...] = got13[eh]
-    seld[...] = gotd[eh]
-    own(1, start, start)
-    for cp in sel_local():
-        cp.start()
-    for cp in along_z():
-        cp.start()
-    zsend(1, True, start, start)
-    hot_z_landed(zc)
-    for cp in forward_z():
-        cp.start()
-    own(2, start, start)
-    zsend(2, True, start, start)
-
-    for cp in sel_local():
-        cp.wait()
-    hot_z_landed(z1)
-    hot_z_landed(zf)
-    for cp in gather():
-        cp.start()
-    for i in range(3):
-        yy, xx = same_core[i]
-        hot_rows_landed(4 * yy + 2 * xx + c)
-        for cp in to_sibling(i):
+    def build_all():
+        for cp in part_loads():
+            cp.wait()
+        kh = lax.rem(hot_ref[0], 4)
+
+        def build(i, carry):
+            t, b = i // 4, i % 4
+            for par, to13, tod in ((1 - c, give13, gived), (c, pair13.at[c], paird.at[c])):
+                rr = pl.ds(pl.multiple_of((2 * b + par) * r8, r8), r8)
+                rd = pl.ds(pl.multiple_of((2 * b + par) * d8, d8), d8)
+                to13[b, t, :, 0:ff] = part_g[kh, t, rr, :]
+                to13[b, t, :, ff:2 * ff] = part_u[kh, t, rr, :]
+                tod[b, t] = part_d[kh, t, rd, :]
+            return carry
+
+        lax.fori_loop(0, nl * 4, build, 0)
+
+    def merge():
+        landed(pair13.at[1 - c], r_pair.at[0])
+        landed(paird.at[1 - c], r_pair.at[1])
+        core = lax.rem(hot_ref[0] // 4, 2)
+
+        def pick(i, carry):
+            b, t = i // nl, i % nl
+            mine13[b, t] = pair13[core, b, t]
+            mined[b, t] = paird[core, b, t]
+            return carry
+
+        lax.fori_loop(0, nl * 4, pick, 0)
+
+    def run(group):
+        for cp in group:
             cp.start()
+
+    def select():
+        for cp in scatter_local():
+            cp.wait()
+        for yy, xx in same_core:
+            q = 2 * yy + xx
+            landed(got13.at[q], r_hs.at[q, 0])
+            landed(gotd.at[q], r_hs.at[q, 1])
+        owner = lax.div(hot_ref[0], 8)
+        sel13[...] = got13[owner]
+        seld[...] = gotd[owner]
+
+    def sct():
+        run(scatter_local())
+        run(scatter())
+
+    def alongz():
+        run(along_z())
+        run(sel_local())
+
+    def fwd():
+        hot_z_landed(zc)
+        run(forward_z())
+
+    def gat():
+        for cp in sel_local():
+            cp.wait()
+        hot_z_landed(z1)
+        hot_z_landed(zf)
+        run(gather())
+
+    def sib():
+        for i in range(3):
+            yy, xx = same_core[i]
+            hot_rows_landed(4 * yy + 2 * xx + c)
+            run(to_sibling(i))
+
+    steps = dict(load=lambda: run(part_loads()), build=build_all, pair=lambda: run(pair()), merge=merge, scatter=sct,
+                 select=select, alongz=alongz, fwd=fwd, gather=gat, sib=sib)
+    for t in range(nl):
+        steps[f'own{t}'] = functools.partial(own, t, start, start)
+        for p in range(len(CUTS[t])):
+            steps[f'in{t}{p}'] = functools.partial(p1, t, p, start)
+            steps[f'z{t}{p}'] = functools.partial(zsend, t, p, range(3), True, start, start)
+            for m in range(3):
+                steps[f'z{t}{p}{m}'] = functools.partial(zsend, t, p, (m,), True, start, start)
+    for step in ORDER:
+        steps[step]()
 
     for yy in range(2):
         for xx in range(2):
@@ -250,9 +297,10 @@
 
     for t in range(nl):
         own(t, wait, wait_send)
-        p1(t, wait_send)
-        zsend(t, False, wait, wait_send)
-    for group in (scatter(), along_z(), forward_z(), gather(), to_sibling(0), to_sibling(1), to_sibling(2)):
+        for p in range(len(CUTS[t])):
+            p1(t, p, wait_send)
+            zsend(t, p, range(3), False, wait, wait_send)
+    for group in (pair(), scatter(), along_z(), forward_z(), gather(), to_sibling(0), to_sibling(1), to_sibling(2)):
         for cp in group:
             cp.wait_send()
 
@@ -301,6 +349,8 @@
         nl, _, dm, f4 = gate.shape
         ff = f4 // 4
         lay = nl * 4
+        r8, d8 = dm // 8, ff // 8
+        cut = max(map(len, CUTS))
         dma = pltpu.SemaphoreType.DMA
         shapes = [(lay, dm, 2 * ff), (lay, ff, dm)] * 2
         outs = pl.pallas_call(
@@ -310,13 +360,15 @@
             out_specs=[vmem] * 4,
             scratch_shapes=[
                 pltpu.VMEM((4, nl, dm, ff), BF16), pltpu.VMEM((4, nl, dm, ff), BF16), pltpu.VMEM((4, nl, ff, dm), BF16),
-                pltpu.VMEM((nl, dm, 2 * ff), BF16), pltpu.VMEM((nl, ff, dm), BF16),
+                pltpu.VMEM((2, 4, nl, r8, 2 * ff), BF16), pltpu.VMEM((2, 4, nl, d8, dm), BF16),
+                pltpu.VMEM((4, nl, r8, 2 * ff), BF16), pltpu.VMEM((4, nl, d8, dm), BF16),
+                pltpu.VMEM((4, nl, r8, 2 * ff), BF16), pltpu.VMEM((4, nl, d8, dm), BF16),
                 pltpu.VMEM((3, nl, dm, 2 * ff), BF16), pltpu.VMEM((3, nl, ff, dm), BF16),
-                pltpu.VMEM((8, nl, dm // 8, 2 * ff), BF16), pltpu.VMEM((8, nl, ff // 8, dm), BF16),
-                pltpu.VMEM((nl, dm // 8, 2 * ff), BF16), pltpu.VMEM((nl, ff // 8, dm), BF16),
-                dma((2, nl, 3)), dma((2, 2, nl, 3)), dma((3, nl, 2)), dma((8, 2)), dma((3, 2)), dma((7, 2)),
-                dma((3, nl, 2)), dma((lay, 2)), dma((8, 2)), dma((4, 2)), dma((8, 2)),
-                dma((nl, 3)), dma((nl, 2)), dma((4, 3)), dma((4,)),
+                pltpu.VMEM((4, nl, r8, 2 * ff), BF16), pltpu.VMEM((4, nl, d8, dm), BF16),
+                pltpu.VMEM((nl, r8, 2 * ff), BF16), pltpu.VMEM((nl, d8, dm), BF16),
+                dma((2, nl, 3)), dma((2, 2, nl, cut, 3)), dma((3, nl, cut, 2)), dma((2,)), dma((3, 2)), dma((3, 2)), dma((7, 2)),
+                dma((3, nl, cut, 2)), dma((lay, 2)), dma((2,)), dma((4, 2)), dma((4, 2)), dma((8, 2)),
+                dma((nl, 3)), dma((nl, cut, 2)), dma((4, 3)), dma((4,)),
             ],
             compiler_params=pltpu.CompilerParams(has_side_effects=True, vmem_limit_bytes=44 << 20),
             name='exchange',

time: 272 us -> 249 us (0.915)
  the two profiles are of different devices: /device:TPU:7 before, /device:TPU:19 now
where the time goes in v2:
time: 249 us
  Pallas kernels  247 us (99%)
    pallas_call x1, Pallas kernels, body(): pl.pallas_call(functools.partial(exchange_kernel, (nl, dm, ff)), out_shap...  236 us
    pallas_call x1, Pallas kernels, body(): pl.pallas_call(place_kernel, out_shape=[jax.ShapeDtypeStruct((lay, 3, dm,...  11.3 us

profile of v2, /device:TPU:19, one launch (start us, length us, event | category | flops | bytes accessed | tf_op | source)
XLA Modules:
  0.0 248.9 jit_solution(1195098191828509172)
XLA Ops:
  1.3 0.8 copy.7.slots_ref
  2.0 235.6 %exchange.1 = (bf16[12,1024,256]{2,1,0:T(8,128)(2,1)S(1)}, bf16[12,128,1024]{2,1,0:T(8,128)(2,1)S(1)}, bf16[12,1024,256]{2,1,0:T(8,128)(2,1)S(1)}, bf16[12,128,1024]{2,1,0:T(8,128)(2,1)S(1)}) custom-call(s32[1]{0:T(128)S(6)} %copy.8.hot_ref, bf16[3,1,1024,512]{3,2,1,0:T(8,128)(2,1)} %gate.1, bf16[3,1,1024,512]{3,2,1,0:T(8,128)(2,1)} %up.1, ...), custom_call_target="tpu_custom_call" | custom-call | tf_op jit(solution)/shard_map/exchange/pallas_call | solution.py:356
  237.6 11.3 %place.1 = (bf16[12,3,1024,256]{3,2,1,0:T(8,128)(2,1)}, bf16[12,3,128,1024]{3,2,1,0:T(8,128)(2,1)}) custom-call(s32[32,2]{1,0:T(8,128)S(1)} %copy.7.slots_ref, bf16[12,1024,256]{2,1,0:T(8,128)(2,1)S(1)} %get-tuple-element.6.home13, bf16[12,128,1024]{2,1,0:T(8,128)(2,1)S(1)} %get-tuple-element.7.homed, bf16[12,1024,256]{2,1,0:T(8,128)(2,1)S(1)} %get-tuple-element.8.hot13, ...), custom_call_target="tpu_custom_call" | custom-call | tf_op jit(solution)/shard_map/place/pallas_call | solution.py:376

commit v3 on v2

--- a/solution.py
+++ b/solution.py
@@ -9,11 +9,10 @@
 
 MESH = pl.DeviceIdType.MESH
 ORDER = (
-    'load', 'own0', 'in00', 'in01', 'build', 'in02', 'in03', 'pair', 'z00', 'merge', 'scatter', 'in10', 'in11',
-    'in12', 'in13', 'in20', 'in21', 'in22', 'in23', 'z01', 'z02', 'z03', 'select', 'alongz', 'own1', 'z10', 'z11',
-    'fwd', 'z12', 'z13', 'own2', 'gather', 'z20', 'z21', 'z22', 'z23', 'sib',
+    'in00', 'own0', 'in01', 'load', 'zf0', 'in02', 'zf1', 'in03', 'build', 'pair', 'merge', 'scatter', 'in10',
+    'in11', 'in20', 'in21', 'z02', 'z03', 'select', 'alongz', 'z10', 'z11', 'fwd', 'z20', 'gather', 'z21', 'sib',
 )
-CUTS = (((0, 1), (1, 1), (2, 2), (4, 4)), ((0, 2), (2, 2), (4, 2), (6, 2)), ((0, 2), (2, 2), (4, 2), (6, 2)))
+CUTS = (((0, 1), (1, 1), (2, 2), (4, 4)), ((0, 4), (4, 4)), ((0, 4), (4, 4)))
 BF16 = jnp.bfloat16
 
 
@@ -48,6 +47,10 @@
                 (up.at[t, 0, :, cols(k)], dst13.at[:, pl.ds(ff, ff)]),
                 (down.at[t, 0, cols(k), :], dstd))
 
+    start = lambda cp: cp.start()
+    wait_send = lambda cp: cp.wait_send()
+    wait = lambda cp: cp.wait()
+
     def own(t, do_local, do_remote):
         lay = nl * z + t
         for kc in range(2):
@@ -91,32 +94,66 @@
             to(0, 1, 0)
             to(1, 2, 1)
 
-    relays = ((2 * y + 1 - x), (2 * (1 - y) + x), (2 * (1 - y) + 1 - x))
-
-    def zsend(t, p, ms, wait, do_local, do_remote):
+    first = 1 - abs(y - z // 2)
+
+    def soonest(i):
+        m = (i + first) % 3
+        return m, 2 * ((y + (m + 1) // 2) % 2) + (x + 1 - m * (2 - m)) % 2
+
+    def relay(i):
+        up = 1 - z // 2
+        near = z * up + (3 - z) * (1 - up)
+        zd = (3, 2, 1 - near, near)[i]
+        zd = zd * up + (3 - zd) * (1 - up)
+        dx = (zd % 2 + x) % 2
+        dy = (zd // 2 + y) % 2
+        return jnp.logical_or(dx > 0, dy > 0), dy * (1 + dx), zd
+
+    def zfirst(p):
+        r13, rd = rows(0, p)
+        for i in range(3):
+            m, zd = soonest(i)
+            src = (rel13.at[m, 0, r13], reld.at[m, 0, rd])
+            dst = (home13.at[nl * z, r13], homed.at[nl * z, rd])
+            for a in range(2):
+                landed(src[a], r_rel.at[m, 0, p, a])
+
+            @pl.when(zd == z)
+            def _():
+                for a in range(2):
+                    pltpu.make_async_copy(src[a], dst[a], l_rel.at[0, p, a]).start()
+
+            for k in range(3):
+                _, _, zk = relay(k)
+
+                @pl.when(zd == zk)
+                def _():
+                    for a in range(2):
+                        rdma(src[a], dst[a], s_z.at[k, 0, p, a], r_home.at[nl * z, a], (zk, j)).start()
+
+    def zsend(t, p, wait, do_local, do_remote):
         lay = nl * z + t
         r13, rd = rows(t, p)
-        for m in ms:
-            zm = relays[m]
+        for i in range(4):
+            held, m, zd = relay(i)
             src = (rel13.at[m, t, r13], reld.at[m, t, rd])
             dst = (home13.at[lay, r13], homed.at[lay, rd])
-            if wait:
-                for a in range(2):
-                    landed(src[a], r_rel.at[m, t, p, a])
-
-            @pl.when(zm == z)
+
+            @pl.when(held)
             def _():
                 for a in range(2):
-                    do_local(pltpu.make_async_copy(src[a], dst[a], l_rel.at[t, p, a]))
-
-            @pl.when(zm != z)
-            def _():
-                for a in range(2):
-                    do_remote(rdma(src[a], dst[a], s_z.at[m, t, p, a], r_home.at[lay, a], (zm, j)))
-
-    start = lambda cp: cp.start()
-    wait_send = lambda cp: cp.wait_send()
-    wait = lambda cp: cp.wait()
+                    if wait:
+                        landed(src[a], r_rel.at[m, t, p, a])
+                    if i == 3:
+                        do_local(pltpu.make_async_copy(src[a], dst[a], l_rel.at[t, p, a]))
+                    else:
+                        do_remote(rdma(src[a], dst[a], s_z.at[i, t, p, a], r_home.at[lay, a], (zd, j)))
+
+            if wait and t > 0 and p == 0:
+                @pl.when(jnp.logical_not(held))
+                def _():
+                    own(t, start, start)
+
 
     def part_loads():
         for k in range(4):
@@ -271,13 +308,13 @@
 
     steps = dict(load=lambda: run(part_loads()), build=build_all, pair=lambda: run(pair()), merge=merge, scatter=sct,
                  select=select, alongz=alongz, fwd=fwd, gather=gat, sib=sib)
+    for p in range(len(CUTS[0])):
+        steps[f'zf{p}'] = functools.partial(zfirst, p)
     for t in range(nl):
         steps[f'own{t}'] = functools.partial(own, t, start, start)
         for p in range(len(CUTS[t])):
             steps[f'in{t}{p}'] = functools.partial(p1, t, p, start)
-            steps[f'z{t}{p}'] = functools.partial(zsend, t, p, range(3), True, start, start)
-            for m in range(3):
-                steps[f'z{t}{p}{m}'] = functools.partial(zsend, t, p, (m,), True, start, start)
+            steps[f'z{t}{p}'] = functools.partial(zsend, t, p, True, start, start)
     for step in ORDER:
         steps[step]()
 
@@ -299,7 +336,7 @@
         own(t, wait, wait_send)
         for p in range(len(CUTS[t])):
             p1(t, p, wait_send)
-            zsend(t, p, range(3), False, wait, wait_send)
+            zsend(t, p, False, wait, wait_send)
     for group in (pair(), scatter(), along_z(), forward_z(), gather(), to_sibling(0), to_sibling(1), to_sibling(2)):
         for cp in group:
             cp.wait_send()
@@ -308,35 +345,44 @@
 def place_kernel(slots_ref, home13, homed, hot13, hotd, w13, wd, zero13, zerod, sem):
     n = lax.axis_index('stage') * 8 + lax.axis_index('expert')
     nlay = home13.shape[0]
-
-    def home():
-        yield pltpu.make_async_copy(home13, w13.at[:, 0], sem.at[0, 0])
-        yield pltpu.make_async_copy(homed, wd.at[:, 0], sem.at[0, 1])
-
-    for cp in home():
-        cp.start()
-    zero13[...] = jnp.zeros_like(zero13)
-    zerod[...] = jnp.zeros_like(zerod)
-
-    def fill(act):
+    step = nlay // 4
+
+    def put(slot, src13, srcd, act):
+        for i in range(0, nlay, step):
+            ls = pl.ds(i, step)
+            act(pltpu.make_async_copy(src13.at[ls], w13.at[ls, slot], sem.at[slot, i, 0]))
+            act(pltpu.make_async_copy(srcd.at[ls], wd.at[ls, slot], sem.at[slot, i, 1]))
+
+    start = lambda cp: cp.start()
+    wait = lambda cp: cp.wait()
+    put(0, home13, homed, start)
+    used = [slots_ref[h, n] >= 0 for h in range(2)]
+    empty = jnp.logical_not(jnp.logical_and(*used))
+
+    for h in range(2):
+        @pl.when(used[h])
+        def _():
+            put(1 + h, hot13, hotd, start)
+
+    def zeros(h, act):
+        for lay in range(nlay):
+            act(pltpu.make_async_copy(zero13, w13.at[lay, 1 + h], sem.at[3 + h, lay, 0]))
+            act(pltpu.make_async_copy(zerod, wd.at[lay, 1 + h], sem.at[3 + h, lay, 1]))
+
+    @pl.when(empty)
+    def _():
+        zero13[...] = jnp.zeros_like(zero13)
+        zerod[...] = jnp.zeros_like(zerod)
         for h in range(2):
-            used = slots_ref[n, h] >= 0
-
-            @pl.when(used)
-            def _():
-                act(pltpu.make_async_copy(hot13, w13.at[:, 1 + h], sem.at[1 + h, 0]))
-                act(pltpu.make_async_copy(hotd, wd.at[:, 1 + h], sem.at[1 + h, 1]))
-
-            @pl.when(jnp.logical_not(used))
-            def _():
-                for lay in range(nlay):
-                    act(pltpu.make_async_copy(zero13, w13.at[lay, 1 + h], sem.at[3 + h, 2 * lay]))
-                    act(pltpu.make_async_copy(zerod, wd.at[lay, 1 + h], sem.at[3 + h, 2 * lay + 1]))
-
-    fill(lambda cp: cp.start())
-    fill(lambda cp: cp.wait())
-    for cp in home():
-        cp.wait()
+            pl.when(jnp.logical_not(used[h]))(functools.partial(zeros, h, start))
+        for h in range(2):
+            pl.when(jnp.logical_not(used[h]))(functools.partial(zeros, h, wait))
+
+    for h in range(2):
+        @pl.when(used[h])
+        def _():
+            put(1 + h, hot13, hotd, wait)
+    put(0, home13, homed, wait)
 
 
 def solution(mesh):
@@ -378,10 +424,10 @@
             out_shape=[jax.ShapeDtypeStruct((lay, 3, dm, 2 * ff), BF16), jax.ShapeDtypeStruct((lay, 3, ff, dm), BF16)],
             in_specs=[smem] + [vmem] * 4,
             out_specs=[any_spec] * 2,
-            scratch_shapes=[pltpu.VMEM((dm, 2 * ff), BF16), pltpu.VMEM((ff, dm), BF16), dma((5, 2 * lay))],
+            scratch_shapes=[pltpu.VMEM((dm, 2 * ff), BF16), pltpu.VMEM((ff, dm), BF16), dma((5, lay, 2))],
             compiler_params=pltpu.CompilerParams(vmem_limit_bytes=20 << 20),
             name='place',
-        )(slot_map, *outs)
+        )(slot_map.T, *outs)
 
     specs = P('stage', 'expert')
     return jax.shard_map(body, mesh=mesh, in_specs=(specs, specs, specs, P(), P()),

time: 249 us -> 244 us (0.980)
  the two profiles are of different devices: /device:TPU:19 before, /device:TPU:2 now
where the time goes in v3:
time: 244 us; the launch traced here: 242 us
  Pallas kernels  241 us (99%)
    pallas_call x1, Pallas kernels, body(): pl.pallas_call(functools.partial(exchange_kernel, (nl, dm, ff)), out_shap...  230 us
    pallas_call x1, Pallas kernels, body(): pl.pallas_call(place_kernel, out_shape=[jax.ShapeDtypeStruct((lay, 3, dm,...  10.9 us

profile of v3, /device:TPU:2, one launch (start us, length us, event | category | flops | bytes accessed | tf_op | source)
XLA Modules:
  0.0 242.0 jit_solution(18005555757944298058)
XLA Ops:
  1.3 0.0 copy-start
  1.3 229.8 %exchange.1 = (bf16[12,1024,256]{2,1,0:T(8,128)(2,1)S(1)}, bf16[12,128,1024]{2,1,0:T(8,128)(2,1)S(1)}, bf16[12,1024,256]{2,1,0:T(8,128)(2,1)S(1)}, bf16[12,128,1024]{2,1,0:T(8,128)(2,1)S(1)}) custom-call(s32[1]{0:T(128)S(6)} %copy.7.hot_ref, bf16[3,1,1024,512]{3,2,1,0:T(8,128)(2,1)} %gate.1, bf16[3,1,1024,512]{3,2,1,0:T(8,128)(2,1)} %up.1, ...), custom_call_target="tpu_custom_call" | custom-call | tf_op jit(solution)/shard_map/exchange/pallas_call | solution.py:402
  231.1 0.0 copy-done
  231.1 10.9 %place.1 = (bf16[12,3,1024,256]{3,2,1,0:T(8,128)(2,1)}, bf16[12,3,128,1024]{3,2,1,0:T(8,128)(2,1)}) custom-call(s32[2,32]{1,0:T(2,128)S(1)} %bitcast.1, bf16[12,1024,256]{2,1,0:T(8,128)(2,1)S(1)} %get-tuple-element.6.home13, bf16[12,128,1024]{2,1,0:T(8,128)(2,1)S(1)} %get-tuple-element.7.homed, bf16[12,1024,256]{2,1,0:T(8,128)(2,1)S(1)} %get-tuple-element.8.hot13, ...), custom_call_target="tpu_custom_call" | custom-call | tf_op jit(solution)/shard_map/place/pallas_call | solution.py:422
Async XLA Ops:
  1.3 229.8 %copy-start = (s32[32,2]{0,1:T(2,128)S(1)}, s32[32,2]{0,1:T(2,128)}, u32[]{:S(2)}) copy-start(s32[32,2]{0,1:T(2,128)} %param.9) | copy-start | bytes 772

commit v4 on v3

--- a/solution.py
+++ b/solution.py
@@ -10,9 +10,10 @@
 MESH = pl.DeviceIdType.MESH
 ORDER = (
     'in00', 'own0', 'in01', 'load', 'zf0', 'in02', 'zf1', 'in03', 'build', 'pair', 'merge', 'scatter', 'in10',
-    'in11', 'in20', 'in21', 'z02', 'z03', 'select', 'alongz', 'z10', 'z11', 'fwd', 'z20', 'gather', 'z21', 'sib',
+    'in20', 'in21', 'z02', 'z03', 'select', 'alongz', 'z10', 'fwd', 'gather', 'z20', 'z21', 'sib',
 )
-CUTS = (((0, 1), (1, 1), (2, 2), (4, 4)), ((0, 4), (4, 4)), ((0, 4), (4, 4)))
+CUTS = (((0, 1), (1, 1), (2, 2), (4, 4)), ((0, 8),), ((0, 7), (7, 1)))
+DIRECT = ((2, 1),)
 BF16 = jnp.bfloat16
 
 
@@ -29,6 +30,8 @@
     r8 = dm // 8
     d8 = ff // 8
 
+    first = 1 - abs(y - z // 2)
+
     def dev(zz, yy, xx, cc):
         return (zz, 4 * yy + 2 * xx + cc)
 
@@ -75,26 +78,40 @@
     def p1(t, p, do):
         r13, rd = rows(t, p)
 
-        def to(dx, m, slot):
+        def to(dx, m, slot, direct=False, cores=(0, 1)):
             xx = (x + dx) % 2
-            for kc in range(2):
+            lay = nl * z + t
+            dst13, dstd = (home13.at[lay], homed.at[lay]) if direct else (rel13.at[m, t], reld.at[m, t])
+            for kc in cores:
                 k = 2 * xx + kc
-                todo = ((gate.at[t, 0, r13, cols(k)], rel13.at[m, t, r13, pl.ds(0, ff)]),
-                        (up.at[t, 0, r13, cols(k)], rel13.at[m, t, r13, pl.ds(ff, ff)]),
-                        (down.at[t, 0, pl.ds(pl.multiple_of(k * ff + rd.start, d8), rd.size), :], reld.at[m, t, rd]))
+                todo = ((gate.at[t, 0, r13, cols(k)], dst13.at[r13, pl.ds(0, ff)]),
+                        (up.at[t, 0, r13, cols(k)], dst13.at[r13, pl.ds(ff, ff)]),
+                        (down.at[t, 0, pl.ds(pl.multiple_of(k * ff + rd.start, d8), rd.size), :], dstd.at[rd]))
                 for a, (src, dst) in enumerate(todo):
-                    do(rdma(src, dst, s_p1.at[slot, kc, t, p, a], r_rel.at[m, t, p, a // 2], dev(z, c, xx, kc)))
+                    recv = r_home.at[lay, a // 2] if direct else r_rel.at[m, t, p, a // 2]
+                    do(rdma(src, dst, s_p1.at[slot, kc, t, p, a], recv, dev(zt if direct else z, c, xx, kc)))
 
         @pl.when(c == y)
         def _():
             to(1, 0, 0)
 
+        if (t, p) in DIRECT:
+            @pl.when(jnp.logical_and(c != y, first == 1))
+            def _():
+                to(0, 1, 0)
+
+            @pl.when(jnp.logical_and(c != y, first == 0))
+            def _():
+                to(0, 1, 0, direct=True, cores=(0,))
+                to(0, 1, 0, cores=(1,))
+        else:
+            @pl.when(c != y)
+            def _():
+                to(0, 1, 0)
+
         @pl.when(c != y)
         def _():
-            to(0, 1, 0)
             to(1, 2, 1)
-
-    first = 1 - abs(y - z // 2)
 
     def soonest(i):
         m = (i + first) % 3
@@ -136,6 +153,9 @@
         r13, rd = rows(t, p)
         for i in range(4):
             held, m, zd = relay(i)
+            own_here = jnp.logical_not(held)
+            if (t, p) in DIRECT:
+                held = jnp.logical_and(held, jnp.logical_or(m != 1, jnp.logical_or(first == 0, c == 1)))
             src = (rel13.at[m, t, r13], reld.at[m, t, rd])
             dst = (home13.at[lay, r13], homed.at[lay, rd])
 
@@ -150,7 +170,7 @@
                         do_remote(rdma(src[a], dst[a], s_z.at[i, t, p, a], r_home.at[lay, a], (zd, j)))
 
             if wait and t > 0 and p == 0:
-                @pl.when(jnp.logical_not(held))
+                @pl.when(own_here)
                 def _():
                     own(t, start, start)
 

time: 244 us -> 243 us (level)
  no operation moved by 1% of the time
where the time goes in v4:
time: 243 us
  Pallas kernels  242 us (100%)
    pallas_call x1, Pallas kernels, body(): pl.pallas_call(functools.partial(exchange_kernel, (nl, dm, ff)), out_shap...  231 us
    pallas_call x1, Pallas kernels, body(): pl.pallas_call(place_kernel, out_shape=[jax.ShapeDtypeStruct((lay, 3, dm,...  10.9 us

profile of v4, /device:TPU:2, one launch (start us, length us, event | category | flops | bytes accessed | tf_op | source)
XLA Modules:
  0.0 243.1 jit_solution(6797181847243548307)
XLA Ops:
  1.3 0.0 copy-start
  1.3 230.9 %exchange.1 = (bf16[12,1024,256]{2,1,0:T(8,128)(2,1)S(1)}, bf16[12,128,1024]{2,1,0:T(8,128)(2,1)S(1)}, bf16[12,1024,256]{2,1,0:T(8,128)(2,1)S(1)}, bf16[12,128,1024]{2,1,0:T(8,128)(2,1)S(1)}) custom-call(s32[1]{0:T(128)S(6)} %copy.7.hot_ref, bf16[3,1,1024,512]{3,2,1,0:T(8,128)(2,1)} %gate.1, bf16[3,1,1024,512]{3,2,1,0:T(8,128)(2,1)} %up.1, ...), custom_call_target="tpu_custom_call" | custom-call | tf_op jit(solution)/shard_map/exchange/pallas_call | solution.py:422
  232.2 0.0 copy-done
  232.2 10.9 %place.1 = (bf16[12,3,1024,256]{3,2,1,0:T(8,128)(2,1)}, bf16[12,3,128,1024]{3,2,1,0:T(8,128)(2,1)}) custom-call(s32[2,32]{1,0:T(2,128)S(1)} %bitcast.1, bf16[12,1024,256]{2,1,0:T(8,128)(2,1)S(1)} %get-tuple-element.6.home13, bf16[12,128,1024]{2,1,0:T(8,128)(2,1)S(1)} %get-tuple-element.7.homed, bf16[12,1024,256]{2,1,0:T(8,128)(2,1)S(1)} %get-tuple-element.8.hot13, ...), custom_call_target="tpu_custom_call" | custom-call | tf_op jit(solution)/shard_map/place/pallas_call | solution.py:442
Async XLA Ops:
  1.3 230.9 %copy-start = (s32[32,2]{0,1:T(2,128)S(1)}, s32[32,2]{0,1:T(2,128)}, u32[]{:S(2)}) copy-start(s32[32,2]{0,1:T(2,128)} %param.9) | copy-start | bytes 772
